TPU v7x, 128 devices: a whole 4x4x4 slice. The times are simulated.
128 devices in a mesh: row: 8 (over z, core), col: 16 (over y, x).
Axes of the slice: x: 4, y: 4, z: 4, core: 2. Of those that a mesh axis runs over, the one named last changes fastest.
Arguments:
- ainv_anc: bfloat16 [24576, 24576], P('row', 'col'), may hold values from -6 to 6
- l_panel: bfloat16 [1536, 24576], P('col', 'row'), may hold values from -0.078125 to 0.078125
- diag_inv: float32 [1536, 768], P('col', 'row'), may hold values from -6 to 6
- struct_mask: int32 [2, 192], replicated, may hold values 0 or 1
- pieces: float32 [24576, 32, 128], P(('row', 'col')), may hold values from -6 to 6
- tile_owner: int32 [24576, 1], P(('row', 'col')), may hold values from 0 to 127; in each aligned block of 192 rows (0 to 191, 192 to 383, ...) at most 3 rows name the same one
Outputs:
- ainv_upper: bfloat16 [1536, 24576], P('col', 'row')
- ainv_diag: float32 [1536, 768], P('col', 'row')
- moved: float32 [49152, 32, 128], P(('row', 'col'))
Inputs may be any that keep to these rules, and one draw needn't show every extreme that they name: `tile_owner`: among the 192 pieces of one device no owner is named more than 3 times, a bound that some block reaches.
All inputs are finite; a program needn't handle non-finite values.
Results may differ from a plain program's by a relative error of at most 0.015.
Values may be sent and summed in bfloat16 or wider, within the bound.
A program may use at most 128 MiB of HBM per device.

v0:
```python
import jax
import jax.numpy as jnp
from jax import lax
from jax.sharding import PartitionSpec as P

W = 768
AB = 128
SLOT = 3


def broadcast(value, axis, root):
    mine = lax.axis_index(axis) == root
    return lax.psum(jnp.where(mine, value, jnp.zeros_like(value)), axis)


def cut_along(value, dim, count):
    before, after = (value.shape[:dim], value.shape[dim + 1 :])
    return jnp.moveaxis(value.reshape(*before, count, -1, *after), dim, 0)


def sum_at_owner(value, axis, dim):
    parts = cut_along(value, dim, lax.axis_size(axis))
    arrived = lax.all_to_all(parts, axis, split_axis=0, concat_axis=0, tiled=True)
    return arrived.astype(jnp.float32).sum(axis=0)


def joined_along(parts, dim):
    shape = list(parts.shape[1:])
    shape[dim] *= parts.shape[0]
    return jnp.moveaxis(parts, 0, dim).reshape(shape)


def joined_exchange(value, axis, axes, splits, concats):
    sizes = [lax.axis_size(a) for a in axes]
    parts = cut_along(value, splits[0], sizes[0])
    parts = jnp.moveaxis(cut_along(parts, splits[1] + 1, sizes[1]), 0, 1)
    inside = parts.shape[2:]
    parts = parts.reshape(-1, *inside)
    parts = lax.all_to_all(parts, axis, split_axis=0, concat_axis=0, tiled=True)
    parts = joined_along(parts.reshape(*sizes, *inside), concats[0] + 1)
    return joined_along(parts, concats[1])


def local(ainv_anc, l_panel, diag_inv, struct_mask, pieces, tile_owner):
    row_devices = lax.axis_size("row")
    col_devices = lax.axis_size("col")
    row_index = lax.axis_index("row")
    col_index = lax.axis_index("col")
    slab_rows = l_panel.shape[0]
    local_rows = l_panel.shape[1]
    cross_width = ainv_anc.shape[1]
    group_ratio = col_devices // row_devices
    supernode = col_index * slab_rows // W
    block_count = local_rows // AB
    keep_blocks = lax.dynamic_slice(
        struct_mask, (supernode, row_index * block_count), (1, block_count)
    )
    keep_rows = (
        jnp.broadcast_to(keep_blocks[:, :, None], (1, block_count, AB)).reshape(1, local_rows) > 0
    )
    masked = jnp.where(keep_rows, l_panel, jnp.zeros_like(l_panel))
    gathered = lax.all_gather(masked, "col", axis=0, tiled=True)
    offset = col_index % group_ratio * cross_width
    own_cross = lax.dynamic_slice_in_dim(gathered, offset, cross_width, 1)
    cross_rows = broadcast(own_cross, "row", col_index // group_ratio)
    product = lax.psum_scatter(
        lax.dot_general(
            cross_rows, ainv_anc, (((1,), (1,)), ((), ())), preferred_element_type=jnp.float32
        ).astype(jnp.bfloat16),
        "col",
        scatter_dimension=0,
        tiled=True,
    ).astype(jnp.float32)
    upper_rows = jnp.where(keep_rows, -product, jnp.zeros_like(product)).astype(jnp.bfloat16)
    own_block = lax.dynamic_slice_in_dim(gathered, supernode * W, W, 0)
    diag_part = lax.dot_general(
        upper_rows, own_block, (((1,), (1,)), ((), ())), preferred_element_type=jnp.float32
    )
    summed = sum_at_owner(diag_part.astype(jnp.bfloat16), "row", 1)
    ainv_diag = diag_inv - summed
    devices_all = row_devices * col_devices
    owners = tile_owner[:, 0]
    onehot = (owners[:, None] == jnp.arange(devices_all, dtype=jnp.int32)[None, :]).astype(
        jnp.int32
    )
    earlier = jnp.cumsum(onehot, axis=0) - onehot
    rank_in_dest = jnp.sum(earlier * onehot, axis=1)
    slot_index = owners * SLOT + rank_in_dest
    piece_rows = pieces.shape[1]
    piece_cols = pieces.shape[2]
    buffer = (
        jnp.zeros((devices_all * SLOT, piece_rows, piece_cols), jnp.float32)
        .at[slot_index]
        .set(pieces)
    )
    shaped = buffer.reshape(row_devices, col_devices, SLOT, piece_rows, piece_cols)
    arrived = joined_exchange(
        shaped.astype(jnp.bfloat16), ("row", "col"), ("row", "col"), (0, 1), (0, 1)
    ).astype(shaped.dtype)
    moved_pieces = arrived.reshape(devices_all * SLOT, piece_rows, piece_cols)
    return (upper_rows, ainv_diag, moved_pieces)


def solution(mesh):
    in_specs = (
        P("row", "col"),
        P("col", "row"),
        P("col", "row"),
        P(),
        P(("row", "col"), None, None),
        P(("row", "col"), None),
    )
    out_specs = (P("col", "row"), P("col", "row"), P(("row", "col"), None, None))
    return jax.shard_map(local, mesh=mesh, in_specs=in_specs, out_specs=out_specs, check_vma=False)
```

profile of v0, /device:TPU:1, one launch (start us, length us, event | category | flops | bytes accessed | tf_op | source)
XLA Modules:
  0.0 332.0 jit_solution(8603867656916050667)
XLA Ops:
  7.2 0.0 all-gather.2.cloned.1.call-start
  7.2 0.8 compare_bitcast_fusion
  8.0 0.1 broadcast_bitcast_fusion
  8.1 1.9 broadcast_select_fusion
  10.0 0.0 all-gather.2.cloned.1.call-update
  10.0 0.0 all-reduce.3.cloned.1.call-start
  10.1 79.1 %all-gather.2.cloned.1.call-done = bf16[1536,3072]{1,0:T(8,128)(2,1)} async-done(((bf16[96,3072]{1,0:T(8,128)(2,1)}), bf16[1536,3072]{1,0:T(8,128)(2,1)}) %all-gather.2.cloned.1.call-update) | async-done | bytes 9437200 | tf_op jit(solution)/shard_map/all_gather | solution.py:62
  89.2 5.3 %dynamic-slice_select_fusion = bf16[1536,1536]{1,0:T(8,128)(2,1)} fusion(bf16[1536,3072]{1,0:T(8,128)(2,1)} %all-gather.2.cloned.1.call-done, s32[]{:T(128)S(6)} %select_n.53, pred[]{:T(512)S(6)} %eq.27), kind=kLoop, calls=%fused_computation.4 | loop fusion | flops 2359296 | bytes 9437189 | tf_op jit(solution)/shard_map/jit(_where)/select_n | solution.py:13
  94.5 0.0 all-reduce.3.cloned.1.call-update
  94.5 0.0 reduce-scatter.2.cloned.1.call-start
  94.6 72.9 %all-reduce.3.cloned.1.call-done = bf16[1536,1536]{1,0:T(8,128)(2,1)} async-done(((bf16[1536,1536]{1,0:T(8,128)(2,1)}), bf16[1536,1536]{1,0:T(8,128)(2,1)}) %all-reduce.3.cloned.1.call-update) | async-done | bytes 4718608 | tf_op jit(solution)/shard_map/psum | solution.py:13
  167.5 20.3 %convolution_convert_fusion = bf16[1536,3072]{1,0:T(8,128)(2,1)} fusion(bf16[1536,1536]{1,0:T(8,128)(2,1)} %all-reduce.3.cloned.1.call-done, bf16[3072,1536]{1,0:T(8,128)(2,1)} %param.6), kind=kOutput, calls=%fused_computation.1 | convolution fusion | flops 14500233216 | bytes 23592960 | tf_op jit(solution)/shard_map/dot_general | solution.py:67
  187.8 0.0 copy-start.3
  187.8 0.0 reduce-scatter.2.cloned.1.call-update
  187.8 0.0 copy-start
  187.8 0.6 copy-done.3
  188.5 0.1 iota_compare_fusion
  188.6 0.1 fusion.5
  188.8 0.2 fusion.8
  189.0 3.5 %broadcast_in_dim.39 = f32[384,32,128]{2,1,0:T(8,128)} broadcast(f32[]{:T(128)} %constant.65.clone.1), dimensions={} | broadcast | bytes 6291460 | tf_op jit(solution)/shard_map/broadcast_in_dim | solution.py:92
  192.5 0.0 copy-done
  192.5 23.5 %scatter_fusion = f32[384,32,128]{2,1,0:T(8,128)} fusion(f32[384,32,128]{2,1,0:T(8,128)} %broadcast_in_dim.39, s32[192]{0:T(256)S(1)} %bitcast.46, f32[192,32,128]{2,1,0:T(8,128)S(1)} %copy-done), kind=kCustom, calls=%fused_computation | custom fusion | bytes 9437952 | tf_op jit(solution)/shard_map/scatter | solution.py:94
  216.0 5.3 %convert_element_type.54 = bf16[384,32,128]{2,1,0:T(8,128)(2,1)} convert(f32[384,32,128]{2,1,0:T(8,128)} %scatter_fusion) | non-fusion elementwise | flops 1572864 | bytes 9437184 | tf_op jit(solution)/shard_map/convert_element_type | solution.py:98
  221.3 9.8 %all-to-all-start.1 = ((bf16[128,1,1,3,32,128]{5,4,3,2,1,0:T(8,128)(2,1)}), bf16[128,1,1,3,32,128]{5,4,3,2,1,0:T(8,128)(2,1)S(1)}, u32[]{:S(2)}, u32[]{:S(2)}) async-start(bf16[128,1,1,3,32,128]{5,4,3,2,1,0:T(8,128)(2,1)} %bitcast.38), calls=%async_computation.2 | async-start | bytes 6291456 | tf_op jit(solution)/shard_map/all_to_all | solution.py:39
  231.2 74.3 %reduce-scatter.2.cloned.1.call-done = bf16[96,3072]{1,0:T(8,128)(2,1)} async-done(((bf16[1536,3072]{1,0:T(8,128)(2,1)}), bf16[96,3072]{1,0:T(8,128)(2,1)}) %reduce-scatter.2.cloned.1.call-update) | async-done | bytes 589840 | tf_op jit(solution)/shard_map/reduce_scatter | solution.py:66
  305.5 1.2 select_convert_fusion
  306.7 0.0 copy-start.1
  306.7 0.8 copy-done.1
  307.5 3.9 %fusion.2 = bf16[96,768]{1,0:T(8,128)(2,1)S(1)} fusion(bf16[96,3072]{1,0:T(8,128)(2,1)S(1)} %select_convert_fusion, bf16[1536,3072]{1,0:T(8,128)(2,1)} %all-gather.2.cloned.1.call-done, s32[]{:T(128)S(6)} %select_n.56), kind=kOutput, calls=%fused_computation.7 | convolution fusion | flops 453058560 | bytes 5455876 | tf_op jit(solution)/shard_map/dot_general | solution.py:76
  311.5 0.2 reshape.62
  311.7 0.7 copy.18
  312.4 0.0 all-to-all-done.1
  312.4 6.5 %all-to-all-start = ((bf16[8,96,96]{2,1,0:T(8,128)(2,1)}), bf16[8,96,96]{2,1,0:T(8,128)(2,1)S(1)}, u32[]{:S(2)}, u32[]{:S(2)}) async-start(bf16[8,96,96]{2,1,0:T(8,128)(2,1)} %bitcast.34), calls=%async_computation.1 | async-start | bytes 393216 | tf_op jit(solution)/shard_map/all_to_all | solution.py:23
  318.9 0.0 copy-start.2
  318.9 3.8 %bitcast_convert_fusion = f32[384,32,128]{2,1,0:T(8,128)} fusion(bf16[128,1,1,3,32,128]{5,4,3,2,1,0:T(8,128)(2,1)S(1)} %all-to-all-done.1), kind=kLoop, calls=%fused_computation.5 | loop fusion | flops 1572864 | bytes 9437184 | tf_op jit(solution)/shard_map/convert_element_type | solution.py:99
  322.7 2.1 all-to-all-done
  324.8 0.0 copy-done.2
  324.8 0.6 sub.15
  (9 shorter events, 0.1 us)
Async XLA Ops:
  7.2 82.0 %all-gather.2.cloned.1.call-start = ((), (), s32[]{:S(2)}) async-start(), calls=%async_computation.3 | async-start | bytes 10027008 | tf_op jit(solution)/shard_map/all_gather | solution.py:62
  10.0 157.4 %all-reduce.3.cloned.1.call-start = ((), (), s32[]{:S(2)}) async-start(), calls=%async_computation.4 | async-start | bytes 9437184 | tf_op jit(solution)/shard_map/psum | solution.py:13
  94.5 211.0 %reduce-scatter.2.cloned.1.call-start = ((), (), s32[]{:S(2)}) async-start(), calls=%async_computation.5 | async-start | bytes 10027008 | tf_op jit(solution)/shard_map/reduce_scatter | solution.py:66
  187.8 0.7 copy-start.3
  187.8 4.7 %copy-start = (f32[192,32,128]{2,1,0:T(8,128)S(1)}, f32[192,32,128]{2,1,0:T(8,128)}, u32[]{:S(2)}) copy-start(f32[192,32,128]{2,1,0:T(8,128)} %param.10) | copy-start | bytes 9437188
  221.3 91.1 %all-to-all-start.1 = ((bf16[128,1,1,3,32,128]{5,4,3,2,1,0:T(8,128)(2,1)}), bf16[128,1,1,3,32,128]{5,4,3,2,1,0:T(8,128)(2,1)S(1)}, u32[]{:S(2)}, u32[]{:S(2)}) async-start(bf16[128,1,1,3,32,128]{5,4,3,2,1,0:T(8,128)(2,1)} %bitcast.38), calls=%async_computation.2 | async-start | bytes 6291456 | tf_op jit(solution)/shard_map/all_to_all | solution.py:39
  306.7 0.8 copy-start.1
  312.4 12.3 %all-to-all-start = ((bf16[8,96,96]{2,1,0:T(8,128)(2,1)}), bf16[8,96,96]{2,1,0:T(8,128)(2,1)S(1)}, u32[]{:S(2)}, u32[]{:S(2)}) async-start(bf16[8,96,96]{2,1,0:T(8,128)(2,1)} %bitcast.34), calls=%async_computation.1 | async-start | bytes 393216 | tf_op jit(solution)/shard_map/all_to_all | solution.py:23
  318.9 5.9 %copy-start.2 = (f32[96,96]{1,0:T(8,128)S(1)}, f32[96,96]{1,0:T(8,128)}, u32[]{:S(2)}) copy-start(f32[96,96]{1,0:T(8,128)} %param.8) | copy-start | bytes 110596
Sparse Core Ops, SparseCore 0:
  10.7 78.4 all-gather.1
  94.6 72.7 all-reduce.2
  187.9 117.5 reduce-scatter.1
where the time goes:
time: 333 us; the launch traced here: 332 us
  waiting for transfers between devices  228 us (68%)
  local copies, waits for them, and re-layouts  29.5 us (9%)
  matrix products  24.3 us (7%)
  other arithmetic  19.5 us (6%)
  starting transfers between devices  16.4 us (5%)
  between operations  13.9 us (4%)
    all_gather x1, waiting for transfers between devices, local(): gathered = lax.all_gather(masked, 'col', axis=0, tiled=True)  79.1 us
    reduce_scatter x1, waiting for transfers between devices, local(): lax.psum_scatter(lax.dot_general(cross_rows, ainv_anc, (((1,), (1,)), (()...  74.3 us
    psum x1, waiting for transfers between devices, broadcast(): return lax.psum(jnp.where(mine, value, jnp.zeros_like(value)), axis)  72.9 us
    scatter x1, local copies, waits for them, and re-layouts, local(): buffer = jnp.zeros((devices_all * SLOT, piece_rows, piece_cols), jnp.floa...  23.5 us
    dot_general x1, matrix products, local(): lax.dot_general(cross_rows, ainv_anc, (((1,), (1,)), ((), ())), preferred...  20.3 us
    all_to_all x1, starting transfers between devices, joined_exchange(): parts = lax.all_to_all(parts, axis, split_axis=0, concat_axis=0, tiled=True)  9.85 us
  transfers between devices with their start and end apart: 5, of which 4 were waited for; matrix products, arithmetic and copies ran while one was open for 13% of the time, Pallas kernels for 0%

commit v1 on v0

--- a/solution.py
+++ b/solution.py
@@ -6,6 +6,27 @@
 W = 768
 AB = 128
 SLOT = 3
+
+
+def gather_around(value, axis, dim):
+    size, here, rows = (lax.axis_size(axis), lax.axis_index(axis), value.shape[dim])
+    right = [(i, (i + 1) % size) for i in range(size)]
+    behind = [(i, (i - 1) % size) for i in range(size)]
+    whole = jnp.zeros((*value.shape[:dim], size * rows, *value.shape[dim + 1 :]), value.dtype)
+    whole = lax.dynamic_update_slice_in_dim(whole, value, here * rows, axis=dim)
+    from_left = from_right = value
+    half = size // 2
+    for step in range(1, half + 1):
+        from_left = lax.ppermute(from_left, axis, right)
+        whole = lax.dynamic_update_slice_in_dim(
+            whole, from_left, (here - step) % size * rows, axis=dim
+        )
+        if step < size - half:
+            from_right = lax.ppermute(from_right, axis, behind)
+            whole = lax.dynamic_update_slice_in_dim(
+                whole, from_right, (here + step) % size * rows, axis=dim
+            )
+    return whole
 
 
 def broadcast(value, axis, root):
@@ -59,7 +80,7 @@
         jnp.broadcast_to(keep_blocks[:, :, None], (1, block_count, AB)).reshape(1, local_rows) > 0
     )
     masked = jnp.where(keep_rows, l_panel, jnp.zeros_like(l_panel))
-    gathered = lax.all_gather(masked, "col", axis=0, tiled=True)
+    gathered = gather_around(masked, "col", 0)
     offset = col_index % group_ratio * cross_width
     own_cross = lax.dynamic_slice_in_dim(gathered, offset, cross_width, 1)
     cross_rows = broadcast(own_cross, "row", col_index // group_ratio)

time: 333 us -> 383 us (1.15)
  starting transfers between devices: 16.4 us -> 51.1 us
  local copies, waits for them, and re-layouts: 29.5 us -> 47.3 us
    all_gather x1 -> x0, waiting for transfers between devices: 79.1 us -> none  [local(): gathered = lax.all_gather(masked, 'col', axis=0, tiled=True)]
    ppermute x0 -> x15, waiting for transfers between devices: none -> 72.9 us  [the longest x8 72.9 us: gather_around(): from_left = lax.ppermute(from_left, axis, right)]
    ppermute x0 -> x15, starting transfers between devices: none -> 34.5 us  [the longest x7 32.4 us: gather_around(): from_right = lax.ppermute(from_right, axis, behind)]
    dynamic_update_slice x0 -> x15, local copies, waits for them, and re-layouts: none -> 12.9 us  [the longest x8 6.86 us: gather_around(): lax.dynamic_update_slice_in_dim(whole, from_left, (here - step) % size *...]
    broadcast_in_dim x0 -> x1, local copies, waits for them, and re-layouts: none -> 4.84 us  [gather_around(): jnp.zeros((*value.shape[:dim], size * rows, *value.shape[dim + 1:]), valu...]
  transfers between devices with their start and end apart: 5 -> 19, of which waited for: 4 -> 11; matrix products, arithmetic and copies ran while one was open for 13% -> 14% of each run, Pallas kernels for 0% -> 0%
where the time goes in v1:
time: 383 us; the launch traced here: 382 us
  waiting for transfers between devices  226 us (59%)
  starting transfers between devices  51.1 us (13%)
  local copies, waits for them, and re-layouts  47.3 us (12%)
  matrix products  24.4 us (6%)
  other arithmetic  18.6 us (5%)
  between operations  14.2 us (4%)
    psum x1, waiting for transfers between devices, broadcast(): return lax.psum(jnp.where(mine, value, jnp.zeros_like(value)), axis)  76.5 us
    reduce_scatter x1, waiting for transfers between devices, local(): lax.psum_scatter(lax.dot_general(cross_rows, ainv_anc, (((1,), (1,)), (()...  74.5 us
    ppermute x8, waiting for transfers between devices, gather_around(): from_left = lax.ppermute(from_left, axis, right)  72.9 us
    ppermute x7, starting transfers between devices, gather_around(): from_right = lax.ppermute(from_right, axis, behind)  32.4 us
    scatter x1, local copies, waits for them, and re-layouts, local(): buffer = jnp.zeros((devices_all * SLOT, piece_rows, piece_cols), jnp.floa...  23.5 us
    dot_general x1, matrix products, local(): lax.dot_general(cross_rows, ainv_anc, (((1,), (1,)), ((), ())), preferred...  20.5 us
    all_to_all x1, starting transfers between devices, joined_exchange(): parts = lax.all_to_all(parts, axis, split_axis=0, concat_axis=0, tiled=True)  9.88 us
  transfers between devices with their start and end apart: 19, of which 11 were waited for; matrix products, arithmetic and copies ran while one was open for 14% of the time, Pallas kernels for 0%

profile of v1, /device:TPU:1, one launch (start us, length us, event | category | flops | bytes accessed | tf_op | source)
XLA Modules:
  0.0 381.6 jit_solution(13570247056892812192)
XLA Ops:
  7.3 0.8 compare_bitcast_fusion
  8.2 4.8 %broadcast_in_dim.39 = bf16[1536,3072]{1,0:T(8,128)(2,1)} broadcast(bf16[]{:T(256)} %constant.142.clone.1), dimensions={} | broadcast | bytes 9437186 | tf_op jit(solution)/shard_map/broadcast_in_dim | solution.py:15
  13.0 1.0 constant_dynamic-update-slice_fusion.15
  14.0 2.0 collective-permute-start
  16.0 3.7 collective-permute-start.1
  19.7 13.0 %collective-permute-done = bf16[96,3072]{1,0:T(8,128)(2,1)S(1)} collective-permute-done((bf16[96,3072]{1,0:T(8,128)(2,1)S(1)}, bf16[96,3072]{1,0:T(8,128)(2,1)S(1)}, u32[]{:S(2)}, u32[]{:S(2)}) %collective-permute-start) | collective-permute-done | bytes 589856 | tf_op jit(solution)/shard_map/ppermute | solution.py:20
  32.7 4.8 %collective-permute-start.3 = (bf16[96,3072]{1,0:T(8,128)(2,1)S(1)}, bf16[96,3072]{1,0:T(8,128)(2,1)S(1)}, u32[]{:S(2)}, u32[]{:S(2)}) collective-permute-start(bf16[96,3072]{1,0:T(8,128)(2,1)S(1)} %collective-permute-done.1), channel_id=1, source_target_pairs={{0,15},{1,0},{2,1},{3,2},{4,3},{5,4},{6,5},{7,6},{8,7},{9,8},{10,9... | collective-permute-start | bytes 1769480 | tf_op jit(solution)/shard_map/ppermute | solution.py:25
  37.5 0.8 constant_dynamic-update-slice_fusion.14
  38.3 0.9 constant_dynamic-update-slice_fusion.13
  39.2 10.4 %collective-permute-done.2 = bf16[96,3072]{1,0:T(8,128)(2,1)S(1)} collective-permute-done((bf16[96,3072]{1,0:T(8,128)(2,1)S(1)}, bf16[96,3072]{1,0:T(8,128)(2,1)S(1)}, u32[]{:S(2)}, u32[]{:S(2)}) %collective-permute-start.2) | collective-permute-done | bytes 589856 | tf_op jit(solution)/shard_map/ppermute | solution.py:20
  49.6 4.8 %collective-permute-start.5 = (bf16[96,3072]{1,0:T(8,128)(2,1)S(1)}, bf16[96,3072]{1,0:T(8,128)(2,1)S(1)}, u32[]{:S(2)}, u32[]{:S(2)}) collective-permute-start(bf16[96,3072]{1,0:T(8,128)(2,1)S(1)} %collective-permute-done.3), channel_id=1, source_target_pairs={{0,15},{1,0},{2,1},{3,2},{4,3},{5,4},{6,5},{7,6},{8,7},{9,8},{10,9... | collective-permute-start | bytes 1769480 | tf_op jit(solution)/shard_map/ppermute | solution.py:25
  54.4 0.9 constant_dynamic-update-slice_fusion.12
  55.3 0.9 constant_dynamic-update-slice_fusion.11
  56.1 9.5 %collective-permute-done.4 = bf16[96,3072]{1,0:T(8,128)(2,1)S(1)} collective-permute-done((bf16[96,3072]{1,0:T(8,128)(2,1)S(1)}, bf16[96,3072]{1,0:T(8,128)(2,1)S(1)}, u32[]{:S(2)}, u32[]{:S(2)}) %collective-permute-start.4) | collective-permute-done | bytes 589856 | tf_op jit(solution)/shard_map/ppermute | solution.py:20
  65.7 4.8 %collective-permute-start.7 = (bf16[96,3072]{1,0:T(8,128)(2,1)S(1)}, bf16[96,3072]{1,0:T(8,128)(2,1)S(1)}, u32[]{:S(2)}, u32[]{:S(2)}) collective-permute-start(bf16[96,3072]{1,0:T(8,128)(2,1)S(1)} %collective-permute-done.5), channel_id=1, source_target_pairs={{0,15},{1,0},{2,1},{3,2},{4,3},{5,4},{6,5},{7,6},{8,7},{9,8},{10,9... | collective-permute-start | bytes 1769480 | tf_op jit(solution)/shard_map/ppermute | solution.py:25
  70.5 0.8 constant_dynamic-update-slice_fusion.10
  71.3 0.9 constant_dynamic-update-slice_fusion.9
  72.2 8.7 %collective-permute-done.6 = bf16[96,3072]{1,0:T(8,128)(2,1)S(1)} collective-permute-done((bf16[96,3072]{1,0:T(8,128)(2,1)S(1)}, bf16[96,3072]{1,0:T(8,128)(2,1)S(1)}, u32[]{:S(2)}, u32[]{:S(2)}) %collective-permute-start.6) | collective-permute-done | bytes 589856 | tf_op jit(solution)/shard_map/ppermute | solution.py:20
  80.9 4.8 %collective-permute-start.9 = (bf16[96,3072]{1,0:T(8,128)(2,1)S(1)}, bf16[96,3072]{1,0:T(8,128)(2,1)S(1)}, u32[]{:S(2)}, u32[]{:S(2)}) collective-permute-start(bf16[96,3072]{1,0:T(8,128)(2,1)S(1)} %collective-permute-done.7), channel_id=1, source_target_pairs={{0,15},{1,0},{2,1},{3,2},{4,3},{5,4},{6,5},{7,6},{8,7},{9,8},{10,9... | collective-permute-start | bytes 1769480 | tf_op jit(solution)/shard_map/ppermute | solution.py:25
  85.7 0.9 constant_dynamic-update-slice_fusion.8
  86.5 0.9 constant_dynamic-update-slice_fusion.7
  87.4 7.8 %collective-permute-done.8 = bf16[96,3072]{1,0:T(8,128)(2,1)S(1)} collective-permute-done((bf16[96,3072]{1,0:T(8,128)(2,1)S(1)}, bf16[96,3072]{1,0:T(8,128)(2,1)S(1)}, u32[]{:S(2)}, u32[]{:S(2)}) %collective-permute-start.8) | collective-permute-done | bytes 589856 | tf_op jit(solution)/shard_map/ppermute | solution.py:20
  95.3 4.8 %collective-permute-start.11 = (bf16[96,3072]{1,0:T(8,128)(2,1)S(1)}, bf16[96,3072]{1,0:T(8,128)(2,1)S(1)}, u32[]{:S(2)}, u32[]{:S(2)}) collective-permute-start(bf16[96,3072]{1,0:T(8,128)(2,1)S(1)} %collective-permute-done.9), channel_id=1, source_target_pairs={{0,15},{1,0},{2,1},{3,2},{4,3},{5,4},{6,5},{7,6},{8,7},{9,8},{10,9... | collective-permute-start | bytes 1769480 | tf_op jit(solution)/shard_map/ppermute | solution.py:25
  100.0 0.9 constant_dynamic-update-slice_fusion.6
  100.9 0.9 constant_dynamic-update-slice_fusion.5
  101.8 7.0 %collective-permute-done.10 = bf16[96,3072]{1,0:T(8,128)(2,1)S(1)} collective-permute-done((bf16[96,3072]{1,0:T(8,128)(2,1)S(1)}, bf16[96,3072]{1,0:T(8,128)(2,1)S(1)}, u32[]{:S(2)}, u32[]{:S(2)}) %collective-permute-start.10) | collective-permute-done | bytes 589856 | tf_op jit(solution)/shard_map/ppermute | solution.py:20
  108.7 4.8 %collective-permute-start.13 = (bf16[96,3072]{1,0:T(8,128)(2,1)S(1)}, bf16[96,3072]{1,0:T(8,128)(2,1)S(1)}, u32[]{:S(2)}, u32[]{:S(2)}) collective-permute-start(bf16[96,3072]{1,0:T(8,128)(2,1)S(1)} %collective-permute-done.11), channel_id=1, source_target_pairs={{0,15},{1,0},{2,1},{3,2},{4,3},{5,4},{6,5},{7,6},{8,7},{9,8},{10,9... | collective-permute-start | bytes 1769480 | tf_op jit(solution)/shard_map/ppermute | solution.py:25
  113.5 0.9 constant_dynamic-update-slice_fusion.4
  114.4 0.9 constant_dynamic-update-slice_fusion.3
  115.3 6.1 %collective-permute-done.12 = bf16[96,3072]{1,0:T(8,128)(2,1)S(1)} collective-permute-done((bf16[96,3072]{1,0:T(8,128)(2,1)S(1)}, bf16[96,3072]{1,0:T(8,128)(2,1)S(1)}, u32[]{:S(2)}, u32[]{:S(2)}) %collective-permute-start.12) | collective-permute-done | bytes 589856 | tf_op jit(solution)/shard_map/ppermute | solution.py:20
  121.4 0.8 constant_dynamic-update-slice_fusion.2
  122.2 0.9 constant_dynamic-update-slice_fusion.1
  123.1 10.3 %collective-permute-done.14 = bf16[96,3072]{1,0:T(8,128)(2,1)S(1)} collective-permute-done((bf16[96,3072]{1,0:T(8,128)(2,1)S(1)}, bf16[96,3072]{1,0:T(8,128)(2,1)S(1)}, u32[]{:S(2)}, u32[]{:S(2)}) %collective-permute-start.14) | collective-permute-done | bytes 589856 | tf_op jit(solution)/shard_map/ppermute | solution.py:20
  133.4 0.8 constant_dynamic-update-slice_fusion
  134.3 5.3 %dynamic-slice_select_fusion = bf16[1536,1536]{1,0:T(8,128)(2,1)} fusion(bf16[1536,3072]{1,0:T(8,128)(2,1)} %constant_dynamic-update-slice_fusion, s32[]{:T(128)S(6)} %select_n.192, pred[]{:T(512)S(6)} %eq.42), kind=kLoop, calls=%fused_computation.4 | loop fusion | flops 2359296 | bytes 9437189 | tf_op jit(solution)/shard_map/jit(_where)/select_n | solution.py:34
  139.9 76.5 %all-reduce.3.cloned.1.call-done = bf16[1536,1536]{1,0:T(8,128)(2,1)} async-done(((bf16[1536,1536]{1,0:T(8,128)(2,1)}), bf16[1536,1536]{1,0:T(8,128)(2,1)}) %all-reduce.3.cloned.1.call-update) | async-done | bytes 4718608 | tf_op jit(solution)/shard_map/psum | solution.py:34
  216.3 20.5 %convolution_convert_fusion = bf16[1536,3072]{1,0:T(8,128)(2,1)} fusion(bf16[1536,1536]{1,0:T(8,128)(2,1)} %all-reduce.3.cloned.1.call-done, bf16[3072,1536]{1,0:T(8,128)(2,1)} %param.6), kind=kOutput, calls=%fused_computation.1 | convolution fusion | flops 14500233216 | bytes 23592960 | tf_op jit(solution)/shard_map/dot_general | solution.py:88
  238.0 3.5 broadcast_in_dim.43
  241.5 23.5 %scatter_fusion = f32[384,32,128]{2,1,0:T(8,128)} fusion(f32[384,32,128]{2,1,0:T(8,128)} %broadcast_in_dim.43, s32[192]{0:T(256)S(1)} %bitcast.46, f32[192,32,128]{2,1,0:T(8,128)S(1)} %copy-done), kind=kCustom, calls=%fused_computation | custom fusion | bytes 9437952 | tf_op jit(solution)/shard_map/scatter | solution.py:115
  265.0 5.3 %convert_element_type.54 = bf16[384,32,128]{2,1,0:T(8,128)(2,1)} convert(f32[384,32,128]{2,1,0:T(8,128)} %scatter_fusion) | non-fusion elementwise | flops 1572864 | bytes 9437184 | tf_op jit(solution)/shard_map/convert_element_type | solution.py:119
  270.3 9.9 %all-to-all-start.1 = ((bf16[128,1,1,3,32,128]{5,4,3,2,1,0:T(8,128)(2,1)}), bf16[128,1,1,3,32,128]{5,4,3,2,1,0:T(8,128)(2,1)S(1)}, u32[]{:S(2)}, u32[]{:S(2)}) async-start(bf16[128,1,1,3,32,128]{5,4,3,2,1,0:T(8,128)(2,1)} %bitcast.38), calls=%async_computation.2 | async-start | bytes 6291456 | tf_op jit(solution)/shard_map/all_to_all | solution.py:60
  280.2 74.5 %reduce-scatter.2.cloned.1.call-done = bf16[96,3072]{1,0:T(8,128)(2,1)} async-done(((bf16[1536,3072]{1,0:T(8,128)(2,1)}), bf16[96,3072]{1,0:T(8,128)(2,1)}) %reduce-scatter.2.cloned.1.call-update) | async-done | bytes 589840 | tf_op jit(solution)/shard_map/reduce_scatter | solution.py:87
  354.8 1.2 select_convert_fusion
  356.0 0.8 copy-done.1
  356.8 3.9 %fusion.2 = bf16[96,768]{1,0:T(8,128)(2,1)S(1)} fusion(bf16[96,3072]{1,0:T(8,128)(2,1)S(1)} %select_convert_fusion, bf16[1536,3072]{1,0:T(8,128)(2,1)} %constant_dynamic-update-slice_fusion, s32[]{:T(128)S(6)} %select_n.195), kind=kOutput, calls=%fused_computation.7 | convolution fusion | flops 453058560 | bytes 5455876 | tf_op jit(solution)/shard_map/dot_general | solution.py:97
  361.7 6.5 %all-to-all-start = ((bf16[8,96,96]{2,1,0:T(8,128)(2,1)}), bf16[8,96,96]{2,1,0:T(8,128)(2,1)S(1)}, u32[]{:S(2)}, u32[]{:S(2)}) async-start(bf16[8,96,96]{2,1,0:T(8,128)(2,1)} %bitcast.34), calls=%async_computation.1 | async-start | bytes 393216 | tf_op jit(solution)/shard_map/all_to_all | solution.py:44
  368.2 3.8 bitcast_convert_fusion
  372.0 2.1 all-to-all-done
  (44 shorter events, 3.2 us)
Async XLA Ops:
  7.2 5.8 %copy-start.2 = (bf16[96,3072]{1,0:T(8,128)(2,1)S(1)}, bf16[96,3072]{1,0:T(8,128)(2,1)}, u32[]{:S(2)}) copy-start(bf16[96,3072]{1,0:T(8,128)(2,1)} %param.7) | copy-start | bytes 1769476
  7.2 209.2 %all-reduce.3.cloned.1.call-start = ((), (), s32[]{:S(2)}) async-start(), calls=%async_computation.3 | async-start | bytes 9437184 | tf_op jit(solution)/shard_map/psum | solution.py:34
  14.0 18.7 %collective-permute-start = (bf16[96,3072]{1,0:T(8,128)(2,1)S(1)}, bf16[96,3072]{1,0:T(8,128)(2,1)S(1)}, u32[]{:S(2)}, u32[]{:S(2)}) collective-permute-start(bf16[96,3072]{1,0:T(8,128)(2,1)S(1)} %get-tuple-element.4), channel_id=1, source_target_pairs={{0,1},{1,2},{2,3},{3,4},{4,5},{5,6},{6,7},{7,8},{8,9},{9,10},{10,1... | collective-permute-start | bytes 1769480 | tf_op jit(solution)/shard_map/ppermute | solution.py:20
  16.0 16.7 %collective-permute-start.1 = (bf16[96,3072]{1,0:T(8,128)(2,1)S(1)}, bf16[96,3072]{1,0:T(8,128)(2,1)S(1)}, u32[]{:S(2)}, u32[]{:S(2)}) collective-permute-start(bf16[96,3072]{1,0:T(8,128)(2,1)S(1)} %get-tuple-element.4), channel_id=1, source_target_pairs={{0,15},{1,0},{2,1},{3,2},{4,3},{5,4},{6,5},{7,6},{8,7},{9,8},{10,9... | collective-permute-start | bytes 1769480 | tf_op jit(solution)/shard_map/ppermute | solution.py:25
  32.7 16.9 %collective-permute-start.2 = (bf16[96,3072]{1,0:T(8,128)(2,1)S(1)}, bf16[96,3072]{1,0:T(8,128)(2,1)S(1)}, u32[]{:S(2)}, u32[]{:S(2)}) collective-permute-start(bf16[96,3072]{1,0:T(8,128)(2,1)S(1)} %collective-permute-done), channel_id=1, source_target_pairs={{0,1},{1,2},{2,3},{3,4},{4,5},{5,6},{6,7},{7,8},{8,9},{9,10},{10,1... | collective-permute-start | bytes 1769480 | tf_op jit(solution)/shard_map/ppermute | solution.py:20
  32.7 16.9 %collective-permute-start.3 = (bf16[96,3072]{1,0:T(8,128)(2,1)S(1)}, bf16[96,3072]{1,0:T(8,128)(2,1)S(1)}, u32[]{:S(2)}, u32[]{:S(2)}) collective-permute-start(bf16[96,3072]{1,0:T(8,128)(2,1)S(1)} %collective-permute-done.1), channel_id=1, source_target_pairs={{0,15},{1,0},{2,1},{3,2},{4,3},{5,4},{6,5},{7,6},{8,7},{9,8},{10,9... | collective-permute-start | bytes 1769480 | tf_op jit(solution)/shard_map/ppermute | solution.py:25
  49.6 16.1 %collective-permute-start.4 = (bf16[96,3072]{1,0:T(8,128)(2,1)S(1)}, bf16[96,3072]{1,0:T(8,128)(2,1)S(1)}, u32[]{:S(2)}, u32[]{:S(2)}) collective-permute-start(bf16[96,3072]{1,0:T(8,128)(2,1)S(1)} %collective-permute-done.2), channel_id=1, source_target_pairs={{0,1},{1,2},{2,3},{3,4},{4,5},{5,6},{6,7},{7,8},{8,9},{9,10},{10,1... | collective-permute-start | bytes 1769480 | tf_op jit(solution)/shard_map/ppermute | solution.py:20
  49.6 16.1 %collective-permute-start.5 = (bf16[96,3072]{1,0:T(8,128)(2,1)S(1)}, bf16[96,3072]{1,0:T(8,128)(2,1)S(1)}, u32[]{:S(2)}, u32[]{:S(2)}) collective-permute-start(bf16[96,3072]{1,0:T(8,128)(2,1)S(1)} %collective-permute-done.3), channel_id=1, source_target_pairs={{0,15},{1,0},{2,1},{3,2},{4,3},{5,4},{6,5},{7,6},{8,7},{9,8},{10,9... | collective-permute-start | bytes 1769480 | tf_op jit(solution)/shard_map/ppermute | solution.py:25
  65.7 15.2 %collective-permute-start.6 = (bf16[96,3072]{1,0:T(8,128)(2,1)S(1)}, bf16[96,3072]{1,0:T(8,128)(2,1)S(1)}, u32[]{:S(2)}, u32[]{:S(2)}) collective-permute-start(bf16[96,3072]{1,0:T(8,128)(2,1)S(1)} %collective-permute-done.4), channel_id=1, source_target_pairs={{0,1},{1,2},{2,3},{3,4},{4,5},{5,6},{6,7},{7,8},{8,9},{9,10},{10,1... | collective-permute-start | bytes 1769480 | tf_op jit(solution)/shard_map/ppermute | solution.py:20
  65.7 15.2 %collective-permute-start.7 = (bf16[96,3072]{1,0:T(8,128)(2,1)S(1)}, bf16[96,3072]{1,0:T(8,128)(2,1)S(1)}, u32[]{:S(2)}, u32[]{:S(2)}) collective-permute-start(bf16[96,3072]{1,0:T(8,128)(2,1)S(1)} %collective-permute-done.5), channel_id=1, source_target_pairs={{0,15},{1,0},{2,1},{3,2},{4,3},{5,4},{6,5},{7,6},{8,7},{9,8},{10,9... | collective-permute-start | bytes 1769480 | tf_op jit(solution)/shard_map/ppermute | solution.py:25
  80.9 14.4 %collective-permute-start.8 = (bf16[96,3072]{1,0:T(8,128)(2,1)S(1)}, bf16[96,3072]{1,0:T(8,128)(2,1)S(1)}, u32[]{:S(2)}, u32[]{:S(2)}) collective-permute-start(bf16[96,3072]{1,0:T(8,128)(2,1)S(1)} %collective-permute-done.6), channel_id=1, source_target_pairs={{0,1},{1,2},{2,3},{3,4},{4,5},{5,6},{6,7},{7,8},{8,9},{9,10},{10,1... | collective-permute-start | bytes 1769480 | tf_op jit(solution)/shard_map/ppermute | solution.py:20
  80.9 14.4 %collective-permute-start.9 = (bf16[96,3072]{1,0:T(8,128)(2,1)S(1)}, bf16[96,3072]{1,0:T(8,128)(2,1)S(1)}, u32[]{:S(2)}, u32[]{:S(2)}) collective-permute-start(bf16[96,3072]{1,0:T(8,128)(2,1)S(1)} %collective-permute-done.7), channel_id=1, source_target_pairs={{0,15},{1,0},{2,1},{3,2},{4,3},{5,4},{6,5},{7,6},{8,7},{9,8},{10,9... | collective-permute-start | bytes 1769480 | tf_op jit(solution)/shard_map/ppermute | solution.py:25
  95.2 13.5 %collective-permute-start.10 = (bf16[96,3072]{1,0:T(8,128)(2,1)S(1)}, bf16[96,3072]{1,0:T(8,128)(2,1)S(1)}, u32[]{:S(2)}, u32[]{:S(2)}) collective-permute-start(bf16[96,3072]{1,0:T(8,128)(2,1)S(1)} %collective-permute-done.8), channel_id=1, source_target_pairs={{0,1},{1,2},{2,3},{3,4},{4,5},{5,6},{6,7},{7,8},{8,9},{9,10},{10,1... | collective-permute-start | bytes 1769480 | tf_op jit(solution)/shard_map/ppermute | solution.py:20
  95.3 13.5 %collective-permute-start.11 = (bf16[96,3072]{1,0:T(8,128)(2,1)S(1)}, bf16[96,3072]{1,0:T(8,128)(2,1)S(1)}, u32[]{:S(2)}, u32[]{:S(2)}) collective-permute-start(bf16[96,3072]{1,0:T(8,128)(2,1)S(1)} %collective-permute-done.9), channel_id=1, source_target_pairs={{0,15},{1,0},{2,1},{3,2},{4,3},{5,4},{6,5},{7,6},{8,7},{9,8},{10,9... | collective-permute-start | bytes 1769480 | tf_op jit(solution)/shard_map/ppermute | solution.py:25
  108.7 12.6 %collective-permute-start.12 = (bf16[96,3072]{1,0:T(8,128)(2,1)S(1)}, bf16[96,3072]{1,0:T(8,128)(2,1)S(1)}, u32[]{:S(2)}, u32[]{:S(2)}) collective-permute-start(bf16[96,3072]{1,0:T(8,128)(2,1)S(1)} %collective-permute-done.10), channel_id=1, source_target_pairs={{0,1},{1,2},{2,3},{3,4},{4,5},{5,6},{6,7},{7,8},{8,9},{9,10},{10,1... | collective-permute-start | bytes 1769480 | tf_op jit(solution)/shard_map/ppermute | solution.py:20
  108.7 13.5 %collective-permute-start.13 = (bf16[96,3072]{1,0:T(8,128)(2,1)S(1)}, bf16[96,3072]{1,0:T(8,128)(2,1)S(1)}, u32[]{:S(2)}, u32[]{:S(2)}) collective-permute-start(bf16[96,3072]{1,0:T(8,128)(2,1)S(1)} %collective-permute-done.11), channel_id=1, source_target_pairs={{0,15},{1,0},{2,1},{3,2},{4,3},{5,4},{6,5},{7,6},{8,7},{9,8},{10,9... | collective-permute-start | bytes 1769480 | tf_op jit(solution)/shard_map/ppermute | solution.py:25
  121.4 12.1 %collective-permute-start.14 = (bf16[96,3072]{1,0:T(8,128)(2,1)S(1)}, bf16[96,3072]{1,0:T(8,128)(2,1)S(1)}, u32[]{:S(2)}, u32[]{:S(2)}) collective-permute-start(bf16[96,3072]{1,0:T(8,128)(2,1)S(1)} %collective-permute-done.12), channel_id=1, source_target_pairs={{0,1},{1,2},{2,3},{3,4},{4,5},{5,6},{6,7},{7,8},{8,9},{9,10},{10,1... | collective-permute-start | bytes 1769480 | tf_op jit(solution)/shard_map/ppermute | solution.py:20
  139.6 215.1 %reduce-scatter.2.cloned.1.call-start = ((), (), s32[]{:S(2)}) async-start(), calls=%async_computation.4 | async-start | bytes 10027008 | tf_op jit(solution)/shard_map/reduce_scatter | solution.py:87
  236.8 0.7 copy-start.4
  236.8 4.7 %copy-start = (f32[192,32,128]{2,1,0:T(8,128)S(1)}, f32[192,32,128]{2,1,0:T(8,128)}, u32[]{:S(2)}) copy-start(f32[192,32,128]{2,1,0:T(8,128)} %param.10) | copy-start | bytes 9437188
  270.3 91.4 %all-to-all-start.1 = ((bf16[128,1,1,3,32,128]{5,4,3,2,1,0:T(8,128)(2,1)}), bf16[128,1,1,3,32,128]{5,4,3,2,1,0:T(8,128)(2,1)S(1)}, u32[]{:S(2)}, u32[]{:S(2)}) async-start(bf16[128,1,1,3,32,128]{5,4,3,2,1,0:T(8,128)(2,1)} %bitcast.38), calls=%async_computation.2 | async-start | bytes 6291456 | tf_op jit(solution)/shard_map/all_to_all | solution.py:60
  280.2 93.9 %copy-start.3 = (f32[96,96]{1,0:T(8,128)S(1)}, f32[96,96]{1,0:T(8,128)}, u32[]{:S(2)}) copy-start(f32[96,96]{1,0:T(8,128)} %param.8) | copy-start | bytes 110596
  356.0 0.8 copy-start.1
  361.7 12.3 %all-to-all-start = ((bf16[8,96,96]{2,1,0:T(8,128)(2,1)}), bf16[8,96,96]{2,1,0:T(8,128)(2,1)S(1)}, u32[]{:S(2)}, u32[]{:S(2)}) async-start(bf16[8,96,96]{2,1,0:T(8,128)(2,1)} %bitcast.34), calls=%async_computation.1 | async-start | bytes 393216 | tf_op jit(solution)/shard_map/all_to_all | solution.py:44
Sparse Core Ops, SparseCore 0:
  139.8 76.5 all-reduce.2
  236.9 117.7 reduce-scatter.1
